TPU v7x, 32 devices: a whole 2x2x4 slice. The times are simulated.
32 devices in a mesh: seq: 8 (over y, x, core), head: 4 (over z).
Axes of the slice: x: 2, y: 2, z: 4, core: 2. Of those that a mesh axis runs over, the one named last changes fastest.
Arguments:
- latent: bfloat16 [1024, 1024], P('seq'), may hold values from -15 to 15
- probe: bfloat16 [1024, 1024], P('seq'), may hold values from -6 to 6
- time_embed: float32 [1024], replicated, may hold values from -6 to 6
- gain_attn: float32 [1024], replicated, may hold values from 0.1 to 1.9
- w_query: bfloat16 [1024, 1024], P(None, 'head'), may hold values from -0.625 to 0.625
- w_key: bfloat16 [1024, 1024], P(None, 'head'), may hold values from -11 to 11
- w_value: bfloat16 [1024, 1024], P(None, 'head'), may hold values from -0.1875 to 0.1875
- w_out: bfloat16 [1024, 1024], P('head'), may hold values from -0.1875 to 0.1875
- gain_mlp: float32 [1024], replicated, may hold values from 0.1 to 1.9
- w_in: bfloat16 [1024, 4096], P(None, 'head'), may hold values from -0.1875 to 0.1875
- w_down: bfloat16 [4096, 1024], P('head'), may hold values from -0.09375 to 0.09375
Outputs:
- latent_end: float32 [1024, 1024], P('seq')
- frame_trace: float32 [1024], P('seq')
- frame_logp: float32 [1024], P('seq')
- mean_logp: float32 [], replicated
All inputs are finite; a program needn't handle non-finite values.
Results may differ from a plain program's by a relative error of at most 0.03.
The roundings to bfloat16 on the way count: a program that leaves them out, or rounds other values in their place, can miss the bound.
Values may be sent and summed in bfloat16 or wider, within the bound.
A program may use at most 64 MiB of HBM per device.

v0:
```python
import math
import jax
import jax.numpy as jnp
from jax import lax
from jax.sharding import PartitionSpec as P

HEAD_DIM = 64
STEPS = 2
EPSILON = 1e-05
GELU_COEF = 0.044715
ROOT_TWO_PI = math.sqrt(2.0 / math.pi)


def norm_pair(values, tangent, norm_gain):
    meansq = jnp.mean(values * values, axis=-1, keepdims=True) + EPSILON
    inverse = lax.rsqrt(meansq)
    inner_mean = jnp.mean(values * tangent, axis=-1, keepdims=True)
    primal = values * inverse * norm_gain
    derived = (tangent * inverse - values * inverse**3 * inner_mean) * norm_gain
    return (primal.astype(jnp.bfloat16), derived.astype(jnp.bfloat16))


def gelu_pair(pre_act, tangent):
    cubic_arg = pre_act + GELU_COEF * pre_act**3
    tanh_value = jnp.tanh(ROOT_TWO_PI * cubic_arg)
    output = 0.5 * pre_act * (1.0 + tanh_value)
    slope_value = 0.5 * (1.0 + tanh_value) + 0.5 * pre_act * (
        1.0 - tanh_value * tanh_value
    ) * ROOT_TWO_PI * (1.0 + 3.0 * GELU_COEF * pre_act * pre_act)
    return (output.astype(jnp.bfloat16), (slope_value * tangent).astype(jnp.bfloat16))


def split_heads(matrix):
    return matrix.reshape(matrix.shape[0], -1, HEAD_DIM)


def score_pair(queries, query_tang, keys, key_tang):
    scale = HEAD_DIM ** (-0.5)
    scores = jnp.einsum("rhd,shd->hrs", queries, keys, preferred_element_type=jnp.float32) * scale
    score_tang = (
        jnp.einsum("rhd,shd->hrs", query_tang, keys, preferred_element_type=jnp.float32)
        + jnp.einsum("rhd,shd->hrs", queries, key_tang, preferred_element_type=jnp.float32)
    ) * scale
    return (scores, score_tang)


def attention(queries, query_tang, keys, vals, key_tang, val_tang):
    rows = queries.shape[0]
    local_cols = queries.shape[1]
    head_count = local_cols // HEAD_DIM
    query_heads = split_heads(queries)
    query_tang_heads = split_heads(query_tang)
    top_start = jnp.full((head_count, rows), -1e30, jnp.float32)
    piece = (
        lax.all_gather(keys, "seq", axis=0, tiled=True),
        lax.all_gather(vals, "seq", axis=0, tiled=True),
    )
    keys_piece = split_heads(piece[0])
    vals_piece = split_heads(piece[1])
    scale = HEAD_DIM ** (-0.5)
    scores = (
        jnp.einsum("rhd,shd->hrs", query_heads, keys_piece, preferred_element_type=jnp.float32)
        * scale
    )
    new_top = jnp.maximum(top_start, jnp.max(scores, axis=-1))
    weights = jnp.exp(scores - new_top[:, :, None])
    total = jnp.sum(weights, axis=-1)
    add_primal = jnp.einsum(
        "hrs,shd->rhd", weights.astype(jnp.bfloat16), vals_piece, preferred_element_type=jnp.float32
    )
    row_top, total, acc_primal = (new_top, total, add_primal)
    piece = (
        lax.all_gather(keys, "seq", axis=0, tiled=True),
        lax.all_gather(vals, "seq", axis=0, tiled=True),
        lax.all_gather(key_tang, "seq", axis=0, tiled=True),
        lax.all_gather(val_tang, "seq", axis=0, tiled=True),
    )
    keys_piece = split_heads(piece[0])
    vals_piece = split_heads(piece[1])
    key_tang_piece = split_heads(piece[2])
    val_tang_piece = split_heads(piece[3])
    scores, score_tang = score_pair(query_heads, query_tang_heads, keys_piece, key_tang_piece)
    weights = jnp.exp(scores - row_top[:, :, None])
    weighted = weights * score_tang
    rounded = weights.astype(jnp.bfloat16)
    rounded_tang = weighted.astype(jnp.bfloat16)
    add_tang = jnp.einsum(
        "hrs,shd->rhd", rounded_tang, vals_piece, preferred_element_type=jnp.float32
    ) + jnp.einsum("hrs,shd->rhd", rounded, val_tang_piece, preferred_element_type=jnp.float32)
    carried = jnp.sum(weighted, axis=-1)
    total_t = jnp.transpose(total)[:, :, None]
    carried_t = jnp.transpose(carried)[:, :, None]
    primal = acc_primal / total_t
    tangent = add_tang / total_t - carried_t / total_t * primal
    return (
        primal.reshape(rows, local_cols).astype(jnp.bfloat16),
        tangent.reshape(rows, local_cols).astype(jnp.bfloat16),
    )


def attend_rows(normed, normed_tang, w_query, w_key, w_value):
    rows = normed.shape[0]
    stacked = jnp.concatenate([normed, normed_tang], axis=0)

    def project(weight):
        both = jnp.dot(stacked, weight, preferred_element_type=jnp.float32).astype(jnp.bfloat16)
        return (both[:rows], both[rows:])

    queries, query_tang = project(w_query)
    keys, key_tang = project(w_key)
    vals, val_tang = project(w_value)
    return attention(queries, query_tang, keys, vals, key_tang, val_tang)


def hidden_pair(normed_mlp, normed_mlp_tang, w_in):
    rows = normed_mlp.shape[0]
    pre_both = jnp.dot(
        jnp.concatenate([normed_mlp, normed_mlp_tang], axis=0),
        w_in,
        preferred_element_type=jnp.float32,
    )
    return gelu_pair(pre_both[:rows], pre_both[rows:])


def whole_field(
    inputs, direction, gain_attn, w_query, w_key, w_value, w_out, gain_mlp, w_in, w_down
):
    rows = inputs.shape[0]
    normed, normed_tang = norm_pair(inputs, direction, gain_attn)
    head_out, head_tang = attend_rows(normed, normed_tang, w_query, w_key, w_value)
    attn_terms = jnp.dot(
        jnp.concatenate([head_out, head_tang], axis=0), w_out, preferred_element_type=jnp.float32
    )
    attn_both = lax.psum(attn_terms, "head")
    attn = attn_both[:rows]
    attn_tang = attn_both[rows:]
    middle = inputs + attn
    middle_tang = direction + attn_tang
    normed_mlp, normed_mlp_tang = norm_pair(middle, middle_tang, gain_mlp)
    activ, activ_tang = hidden_pair(normed_mlp, normed_mlp_tang, w_in)
    mlp_terms = jnp.dot(
        jnp.concatenate([activ, activ_tang], axis=0), w_down, preferred_element_type=jnp.float32
    )
    mlp_both = lax.psum(mlp_terms, "head")
    return (attn + mlp_both[:rows], attn_tang + mlp_both[rows:])


def per_device(
    latent, probe, time_embed, gain_attn, w_query, w_key, w_value, w_out, gain_mlp, w_in, w_down
):
    rows = latent.shape[0]
    width = latent.shape[1]
    state = latent.astype(jnp.float32)
    direction = probe.astype(jnp.float32)
    trace = jnp.zeros((rows,), jnp.float32)
    for euler_step in range(STEPS):
        inputs = state + euler_step / STEPS * time_embed
        field, field_tang = whole_field(
            inputs, direction, gain_attn, w_query, w_key, w_value, w_out, gain_mlp, w_in, w_down
        )
        trace = trace + jnp.sum(direction * field_tang, axis=-1) / (STEPS * width)
        state = state + field / STEPS
    frame_logp = (
        trace - 0.5 * jnp.sum(state * state, axis=-1) / width - 0.5 * math.log(2.0 * math.pi)
    )
    grand_total = lax.psum(jnp.sum(frame_logp), "seq")
    mean_logp = grand_total / (rows * lax.axis_size("seq"))
    return (state, trace, frame_logp, mean_logp)


def solution(mesh):
    return jax.shard_map(
        per_device,
        mesh=mesh,
        in_specs=(
            P("seq", None),
            P("seq", None),
            P(),
            P(),
            P(None, "head"),
            P(None, "head"),
            P(None, "head"),
            P("head", None),
            P(),
            P(None, "head"),
            P("head", None),
        ),
        out_specs=(P("seq", None), P("seq"), P("seq"), P()),
        check_vma=False,
    )
```

profile of v0, /device:TPU:0, one launch (start us, length us, event | category | flops | bytes accessed | tf_op | source)
XLA Modules:
  0.0 390.4 jit_solution(14046082699471560486)
XLA Ops:
  8.1 1.2 fusion.22
  9.3 1.3 fusion.24
  10.7 1.5 convolution_convert_fusion.3
  12.2 11.3 %all_gather.29 = bf16[1024,256]{1,0:T(8,128)(2,1)S(1)} all-gather(bf16[128,256]{1,0:T(8,128)(2,1)S(1)} %get-tuple-element.42), channel_id=1, replica_groups=mesh['seq'=8,'head'=4] {'seq'}, dimensions={0}, use_global_device_ids=true | all-gather | bytes 589824 | tf_op jit(solution)/shard_map/all_gather | solution.py:55
  23.8 1.5 convolution_convert_fusion.4
  25.3 1.8 multiply_reduce_fusion.1
  27.1 1.8 fusion.113
  28.9 9.8 %all_gather.30 = bf16[1024,256]{1,0:T(8,128)(2,1)S(1)} all-gather(bf16[128,256]{1,0:T(8,128)(2,1)S(1)} %get-tuple-element.41), channel_id=1, replica_groups=mesh['seq'=8,'head'=4] {'seq'}, dimensions={0}, use_global_device_ids=true | all-gather | bytes 589824 | tf_op jit(solution)/shard_map/all_gather | solution.py:75
  38.9 1.5 convolution_convert_fusion.5
  40.4 9.9 %all_gather.28 = bf16[1024,256]{1,0:T(8,128)(2,1)} all-gather(bf16[128,256]{1,0:T(8,128)(2,1)S(1)} %get-tuple-element.40), channel_id=1, replica_groups=mesh['seq'=8,'head'=4] {'seq'}, dimensions={0}, use_global_device_ids=true | all-gather | bytes 589824 | tf_op jit(solution)/shard_map/all_gather | solution.py:56
  50.4 1.2 copy.27
  51.6 2.2 fusion
  53.9 2.5 fusion.109
  58.1 10.7 %all_gather.31 = bf16[1024,256]{1,0:T(8,128)(2,1)} all-gather(bf16[128,256]{1,0:T(8,128)(2,1)S(1)} %get-tuple-element.39), channel_id=1, replica_groups=mesh['seq'=8,'head'=4] {'seq'}, dimensions={0}, use_global_device_ids=true | all-gather | bytes 589824 | tf_op jit(solution)/shard_map/all_gather | solution.py:76
  68.8 1.3 copy.30
  70.1 2.2 fusion.12
  72.4 1.4 fusion.77
  73.8 52.3 %all-reduce.5.cloned.1.call-done = f32[256,1024]{1,0:T(8,128)} async-done(((f32[256,1024]{1,0:T(8,128)}), f32[256,1024]{1,0:T(8,128)}) %all-reduce.5.cloned.1.call-update) | async-done | bytes 1048592 | tf_op jit(solution)/shard_map/psum | solution.py:134
  126.1 1.6 multiply_reduce_fusion.7
  127.7 1.2 multiply_convert_fusion.6
  130.5 1.7 fusion.61
  132.3 51.3 %all-reduce.7.cloned.1.call-done = f32[256,1024]{1,0:T(8,128)} async-done(((f32[256,1024]{1,0:T(8,128)}), f32[256,1024]{1,0:T(8,128)}) %all-reduce.7.cloned.1.call-update) | async-done | bytes 1048592 | tf_op jit(solution)/shard_map/psum | solution.py:144
  183.6 1.4 multiply_reduce_fusion.5
  185.7 1.0 convolution_convert_fusion.1
  187.7 11.0 %all_gather.33 = bf16[1024,256]{1,0:T(8,128)(2,1)} all-gather(bf16[128,256]{1,0:T(8,128)(2,1)S(1)} %get-tuple-element.36), channel_id=1, replica_groups=mesh['seq'=8,'head'=4] {'seq'}, dimensions={0}, use_global_device_ids=true | all-gather | bytes 589824 | tf_op jit(solution)/shard_map/all_gather | solution.py:55
  198.7 2.0 copy.32
  201.7 2.9 multiply_reduce_fusion
  204.6 1.8 fusion.114
  206.3 10.7 %all_gather.34 = bf16[1024,256]{1,0:T(8,128)(2,1)} all-gather(bf16[128,256]{1,0:T(8,128)(2,1)S(1)} %get-tuple-element.35), channel_id=1, replica_groups=mesh['seq'=8,'head'=4] {'seq'}, dimensions={0}, use_global_device_ids=true | all-gather | bytes 589824 | tf_op jit(solution)/shard_map/all_gather | solution.py:75
  217.0 2.1 copy.33
  219.1 1.5 fusion.103
  220.6 9.9 %all_gather.32 = bf16[1024,256]{1,0:T(8,128)(2,1)} all-gather(bf16[128,256]{1,0:T(8,128)(2,1)S(1)} %get-tuple-element.34), channel_id=1, replica_groups=mesh['seq'=8,'head'=4] {'seq'}, dimensions={0}, use_global_device_ids=true | all-gather | bytes 589824 | tf_op jit(solution)/shard_map/all_gather | solution.py:56
  230.5 2.1 copy.31
  232.6 2.2 fusion.2
  234.8 2.7 fusion.111
  238.2 1.2 fusion.112
  239.4 1.1 fusion.14
  240.5 10.7 %all_gather.35 = bf16[1024,256]{1,0:T(8,128)(2,1)} all-gather(bf16[128,256]{1,0:T(8,128)(2,1)S(1)} %copy-done.16), channel_id=1, replica_groups=mesh['seq'=8,'head'=4] {'seq'}, dimensions={0}, use_global_device_ids=true | all-gather | bytes 589824 | tf_op jit(solution)/shard_map/all_gather | solution.py:76
  251.2 2.0 copy.34
  253.2 2.4 fusion.13
  255.6 1.4 fusion.81
  257.1 50.3 %all-reduce.9.cloned.1.call-done = f32[256,1024]{1,0:T(8,128)} async-done(((f32[256,1024]{1,0:T(8,128)}), f32[256,1024]{1,0:T(8,128)}) %all-reduce.9.cloned.1.call-update) | async-done | bytes 1048592 | tf_op jit(solution)/shard_map/psum | solution.py:134
  307.4 1.9 multiply_reduce_fusion.4
  311.2 1.7 fusion.69
  312.9 51.3 %all-reduce.11.cloned.1.call-done = f32[256,1024]{1,0:T(8,128)} async-done(((f32[256,1024]{1,0:T(8,128)}), f32[256,1024]{1,0:T(8,128)}) %all-reduce.11.cloned.1.call-update) | async-done | bytes 1048592 | tf_op jit(solution)/shard_map/psum | solution.py:144
  364.2 2.5 multiply_reduce_fusion.2
  366.7 1.1 fusion.101
  367.8 14.3 %psum.39 = f32[]{:T(128)} all-reduce(f32[]{:T(128)} %get-tuple-element.13), channel_id=1, replica_groups=mesh['seq'=8,'head'=4] {'seq'}, use_global_device_ids=true, to_apply=%region_22.0 | all-reduce | flops 1 | bytes 8 | tf_op jit(solution)/shard_map/psum | solution.py:166
  (83 shorter events, 9.8 us)
Async XLA Ops:
  7.2 121.8 %copy-start = (bf16[1024,1024]{1,0:T(8,128)(2,1)S(1)}, bf16[1024,1024]{1,0:T(8,128)(2,1)}, u32[]{:S(2)}) copy-start(bf16[1024,1024]{1,0:T(8,128)(2,1)} %param.20) | copy-start | bytes 6291460
  7.2 118.9 %all-reduce.5.cloned.1.call-start = ((), (), s32[]{:S(2)}) async-start(), calls=%async_computation | async-start | bytes 2097152 | tf_op jit(solution)/shard_map/psum | solution.py:134
  10.6 1.6 copy-start.15
  10.7 13.1 %copy-start.14 = (bf16[128,1024]{1,0:T(8,128)(2,1)}, bf16[128,1024]{1,0:T(8,128)(2,1)S(1)}, u32[]{:S(2)}) copy-start(bf16[128,1024]{1,0:T(8,128)(2,1)S(1)} %get-tuple-element.31) | copy-start | bytes 786436
  51.6 2.2 copy-start.1
  68.8 3.5 copy-start.12
  72.3 53.7 %copy-start.3 = (bf16[128,1024]{1,0:T(8,128)(2,1)S(1)}, bf16[128,1024]{1,0:T(8,128)(2,1)}, u32[]{:S(2)}) copy-start(bf16[128,1024]{1,0:T(8,128)(2,1)} %param.12) | copy-start | bytes 786436
  72.4 55.3 %copy-start.19 = (f32[1024]{0:T(1024)S(1)}, f32[1024]{0:T(1024)}, u32[]{:S(2)}) copy-start(f32[1024]{0:T(1024)} %param.19) | copy-start | bytes 12292
  73.7 109.8 %all-reduce.7.cloned.1.call-start = ((), (), s32[]{:S(2)}) async-start(), calls=%async_computation.1 | async-start | bytes 2097152 | tf_op jit(solution)/shard_map/psum | solution.py:144
  126.1 1.6 copy-start.4
  128.9 1.6 copy-start.5
  132.2 52.8 %copy-start.18 = (f32[1024]{0:T(1024)S(1)}, f32[1024]{0:T(1024)}, u32[]{:S(2)}) copy-start(f32[1024]{0:T(1024)} %param.14) | copy-start | bytes 12292
  132.3 175.1 %all-reduce.9.cloned.1.call-start = ((), (), s32[]{:S(2)}) async-start(), calls=%async_computation.2 | async-start | bytes 2097152 | tf_op jit(solution)/shard_map/psum | solution.py:134
  183.6 1.8 copy-start.20
  183.6 2.1 copy-start.21
  185.0 1.7 copy-start.7
  185.1 1.6 copy-start.22
  200.7 3.8 copy-start.11
  232.6 2.2 copy-start.2
  234.8 3.4 copy-start.10
  238.2 2.3 copy-start.16
  253.2 2.4 copy-start.13
  253.2 2.4 copy-start.17
  257.0 107.2 %all-reduce.11.cloned.1.call-start = ((), (), s32[]{:S(2)}) async-start(), calls=%async_computation.3 | async-start | bytes 2097152 | tf_op jit(solution)/shard_map/psum | solution.py:144
  307.4 1.9 copy-start.9
  309.6 1.6 copy-start.6
  311.2 53.0 %copy-start.8 = (f32[128,1024]{1,0:T(8,128)S(1)}, f32[128,1024]{1,0:T(8,128)}, u32[]{:S(2)}) copy-start(f32[128,1024]{1,0:T(8,128)} %copy-done.7) | copy-start | bytes 1572868
Sparse Core Ops, SparseCore 0:
  73.9 52.1 all-reduce.4
  132.4 51.1 all-reduce.6
  257.1 50.2 all-reduce.8
  313.0 51.1 all-reduce.10
where the time goes:
time: 391 us; the launch traced here: 390 us
  waiting for transfers between devices  205 us (52%)
  blocking collectives  98.5 us (25%)
  matrix products  35.8 us (9%)
  other arithmetic  20.1 us (5%)
  between operations  16 us (4%)
  local copies, waits for them, and re-layouts  14.7 us (4%)
    psum x2, waiting for transfers between devices, whole_field(): attn_both = lax.psum(attn_terms, 'head')  103 us
    psum x2, waiting for transfers between devices, whole_field(): mlp_both = lax.psum(mlp_terms, 'head')  103 us
    all_gather x2, blocking collectives, attention(): lax.all_gather(keys, 'seq', axis=0, tiled=True)  22.4 us
    all_gather x2, blocking collectives, attention(): lax.all_gather(val_tang, 'seq', axis=0, tiled=True)  21.4 us
    all_gather x2, blocking collectives, attention(): lax.all_gather(key_tang, 'seq', axis=0, tiled=True)  20.5 us
    all_gather x2, blocking collectives, attention(): lax.all_gather(vals, 'seq', axis=0, tiled=True)  19.9 us
    psum x1, blocking collectives, per_device(): grand_total = lax.psum(jnp.sum(frame_logp), 'seq')  14.3 us
  transfers between devices with their start and end apart: 4, of which 4 were waited for; matrix products, arithmetic and copies ran while one was open for 0% of the time, Pallas kernels for 0%

commit v1 on v0

--- a/solution.py
+++ b/solution.py
@@ -131,7 +131,11 @@
     attn_terms = jnp.dot(
         jnp.concatenate([head_out, head_tang], axis=0), w_out, preferred_element_type=jnp.float32
     )
-    attn_both = lax.psum(attn_terms, "head")
+    attn_both = attn_terms
+    for hop in (1, 2):
+        attn_both = attn_both + lax.ppermute(
+            attn_both, "head", [(dev, dev ^ hop) for dev in range(4)]
+        )
     attn = attn_both[:rows]
     attn_tang = attn_both[rows:]
     middle = inputs + attn

time: 391 us -> 431 us (1.10)
  waiting for transfers between devices: 205 us -> 242 us
  starting transfers between devices: 0.16 us -> 7.71 us
    ppermute x0 -> x4, waiting for transfers between devices: none -> 140 us  [whole_field(): lax.ppermute(attn_both, 'head', [(dev, dev ^ hop) for dev in range(4)])]
    psum x2 -> x0, waiting for transfers between devices: 103 us -> none  [whole_field(): attn_both = lax.psum(attn_terms, 'head')]
    ppermute x0 -> x4, starting transfers between devices: none -> 7.44 us  [whole_field(): lax.ppermute(attn_both, 'head', [(dev, dev ^ hop) for dev in range(4)])]
  transfers between devices with their start and end apart: 4 -> 6, of which waited for: 4 -> 6; matrix products, arithmetic and copies ran while one was open for 0% -> 0% of each run, Pallas kernels for 0% -> 0%
where the time goes in v1:
time: 431 us; the launch traced here: 430 us
  waiting for transfers between devices  242 us (56%)
  blocking collectives  98.3 us (23%)
  matrix products  33.7 us (8%)
  other arithmetic  16.8 us (4%)
  between operations  16.3 us (4%)
  local copies, waits for them, and re-layouts  15.1 us (4%)
  starting transfers between devices  7.71 us (2%)
    ppermute x4, waiting for transfers between devices, whole_field(): lax.ppermute(attn_both, 'head', [(dev, dev ^ hop) for dev in range(4)])  140 us
    psum x2, waiting for transfers between devices, whole_field(): mlp_both = lax.psum(mlp_terms, 'head')  102 us
    all_gather x2, blocking collectives, attention(): lax.all_gather(keys, 'seq', axis=0, tiled=True)  22.2 us
    all_gather x2, blocking collectives, attention(): lax.all_gather(val_tang, 'seq', axis=0, tiled=True)  21.4 us
    all_gather x2, blocking collectives, attention(): lax.all_gather(key_tang, 'seq', axis=0, tiled=True)  20.5 us
    all_gather x2, blocking collectives, attention(): lax.all_gather(vals, 'seq', axis=0, tiled=True)  19.9 us
    psum x1, blocking collectives, per_device(): grand_total = lax.psum(jnp.sum(frame_logp), 'seq')  14.3 us
  transfers between devices with their start and end apart: 6, of which 6 were waited for; matrix products, arithmetic and copies ran while one was open for 0% of the time, Pallas kernels for 0%

profile of v1, /device:TPU:0, one launch (start us, length us, event | category | flops | bytes accessed | tf_op | source)
XLA Modules:
  0.0 429.7 jit_solution(16617146371123296646)
XLA Ops:
  8.1 1.2 fusion.22
  9.3 1.3 fusion.24
  10.7 1.5 convolution_convert_fusion.3
  12.2 11.3 %all_gather.29 = bf16[1024,256]{1,0:T(8,128)(2,1)S(1)} all-gather(bf16[128,256]{1,0:T(8,128)(2,1)S(1)} %get-tuple-element.42), channel_id=1, replica_groups=mesh['seq'=8,'head'=4] {'seq'}, dimensions={0}, use_global_device_ids=true | all-gather | bytes 589824 | tf_op jit(solution)/shard_map/all_gather | solution.py:55
  23.8 1.5 convolution_convert_fusion.4
  25.3 1.8 multiply_reduce_fusion.1
  27.1 1.8 fusion.113
  28.9 9.8 %all_gather.30 = bf16[1024,256]{1,0:T(8,128)(2,1)S(1)} all-gather(bf16[128,256]{1,0:T(8,128)(2,1)S(1)} %get-tuple-element.41), channel_id=1, replica_groups=mesh['seq'=8,'head'=4] {'seq'}, dimensions={0}, use_global_device_ids=true | all-gather | bytes 589824 | tf_op jit(solution)/shard_map/all_gather | solution.py:75
  38.9 1.5 convolution_convert_fusion.5
  40.4 9.9 %all_gather.28 = bf16[1024,256]{1,0:T(8,128)(2,1)} all-gather(bf16[128,256]{1,0:T(8,128)(2,1)S(1)} %get-tuple-element.40), channel_id=1, replica_groups=mesh['seq'=8,'head'=4] {'seq'}, dimensions={0}, use_global_device_ids=true | all-gather | bytes 589824 | tf_op jit(solution)/shard_map/all_gather | solution.py:56
  50.4 1.2 copy.27
  51.6 2.2 fusion
  53.9 2.5 fusion.109
  58.1 10.7 %all_gather.31 = bf16[1024,256]{1,0:T(8,128)(2,1)} all-gather(bf16[128,256]{1,0:T(8,128)(2,1)S(1)} %get-tuple-element.39), channel_id=1, replica_groups=mesh['seq'=8,'head'=4] {'seq'}, dimensions={0}, use_global_device_ids=true | all-gather | bytes 589824 | tf_op jit(solution)/shard_map/all_gather | solution.py:76
  68.8 1.3 copy.30
  70.1 2.2 fusion.12
  72.7 1.6 collective-permute-start
  74.3 23.8 %collective-permute-done = f32[256,1024]{1,0:T(8,128)S(1)} collective-permute-done((f32[256,1024]{1,0:T(8,128)S(1)}, f32[256,1024]{1,0:T(8,128)S(1)}, u32[]{:S(2)}, u32[]{:S(2)}) %collective-permute-start) | collective-permute-done | bytes 1048608 | tf_op jit(solution)/shard_map/ppermute | solution.py:136
  98.4 2.7 collective-permute-start.1
  101.0 45.3 %collective-permute-done.1 = f32[256,1024]{1,0:T(8,128)S(1)} collective-permute-done((f32[256,1024]{1,0:T(8,128)S(1)}, f32[256,1024]{1,0:T(8,128)S(1)}, u32[]{:S(2)}, u32[]{:S(2)}) %collective-permute-start.1) | collective-permute-done | bytes 1048608 | tf_op jit(solution)/shard_map/ppermute | solution.py:136
  148.7 1.7 fusion.61
  150.7 52.0 %all-reduce.3.cloned.1.call-done = f32[256,1024]{1,0:T(8,128)} async-done(((f32[256,1024]{1,0:T(8,128)}), f32[256,1024]{1,0:T(8,128)}) %all-reduce.3.cloned.1.call-update) | async-done | bytes 1048592 | tf_op jit(solution)/shard_map/psum | solution.py:148
  202.6 1.4 multiply_reduce_fusion.5
  206.7 10.8 %all_gather.33 = bf16[1024,256]{1,0:T(8,128)(2,1)} all-gather(bf16[128,256]{1,0:T(8,128)(2,1)S(1)} %get-tuple-element.36), channel_id=1, replica_groups=mesh['seq'=8,'head'=4] {'seq'}, dimensions={0}, use_global_device_ids=true | all-gather | bytes 589824 | tf_op jit(solution)/shard_map/all_gather | solution.py:55
  217.6 2.0 copy.32
  220.6 2.9 multiply_reduce_fusion
  223.4 1.8 fusion.114
  225.2 10.7 %all_gather.34 = bf16[1024,256]{1,0:T(8,128)(2,1)} all-gather(bf16[128,256]{1,0:T(8,128)(2,1)S(1)} %get-tuple-element.35), channel_id=1, replica_groups=mesh['seq'=8,'head'=4] {'seq'}, dimensions={0}, use_global_device_ids=true | all-gather | bytes 589824 | tf_op jit(solution)/shard_map/all_gather | solution.py:75
  235.9 2.1 copy.33
  238.0 1.5 fusion.103
  239.5 9.9 %all_gather.32 = bf16[1024,256]{1,0:T(8,128)(2,1)} all-gather(bf16[128,256]{1,0:T(8,128)(2,1)S(1)} %get-tuple-element.34), channel_id=1, replica_groups=mesh['seq'=8,'head'=4] {'seq'}, dimensions={0}, use_global_device_ids=true | all-gather | bytes 589824 | tf_op jit(solution)/shard_map/all_gather | solution.py:56
  249.4 2.0 copy.31
  251.5 2.2 fusion.2
  253.7 2.8 fusion.111
  257.1 1.2 fusion.112
  258.3 1.1 fusion.14
  259.4 10.7 %all_gather.35 = bf16[1024,256]{1,0:T(8,128)(2,1)} all-gather(bf16[128,256]{1,0:T(8,128)(2,1)S(1)} %copy-done.18), channel_id=1, replica_groups=mesh['seq'=8,'head'=4] {'seq'}, dimensions={0}, use_global_device_ids=true | all-gather | bytes 589824 | tf_op jit(solution)/shard_map/all_gather | solution.py:76
  270.1 2.0 copy.34
  272.1 2.4 fusion.13
  274.8 1.4 collective-permute-start.2
  276.2 24.1 %collective-permute-done.2 = f32[256,1024]{1,0:T(8,128)S(1)} collective-permute-done((f32[256,1024]{1,0:T(8,128)S(1)}, f32[256,1024]{1,0:T(8,128)S(1)}, u32[]{:S(2)}, u32[]{:S(2)}) %collective-permute-start.2) | collective-permute-done | bytes 1048608 | tf_op jit(solution)/shard_map/ppermute | solution.py:136
  300.5 1.8 collective-permute-start.3
  302.3 46.2 %collective-permute-done.3 = f32[256,1024]{1,0:T(8,128)S(1)} collective-permute-done((f32[256,1024]{1,0:T(8,128)S(1)}, f32[256,1024]{1,0:T(8,128)S(1)}, u32[]{:S(2)}, u32[]{:S(2)}) %collective-permute-start.3) | collective-permute-done | bytes 1048608 | tf_op jit(solution)/shard_map/ppermute | solution.py:136
  351.3 1.7 fusion.69
  353.0 50.4 %all-reduce.5.cloned.1.call-done = f32[256,1024]{1,0:T(8,128)} async-done(((f32[256,1024]{1,0:T(8,128)}), f32[256,1024]{1,0:T(8,128)}) %all-reduce.5.cloned.1.call-update) | async-done | bytes 1048592 | tf_op jit(solution)/shard_map/psum | solution.py:148
  403.4 2.3 multiply_reduce_fusion.2
  405.7 1.1 fusion.101
  406.8 14.3 %psum.23 = f32[]{:T(128)} all-reduce(f32[]{:T(128)} %get-tuple-element.13), channel_id=1, replica_groups=mesh['seq'=8,'head'=4] {'seq'}, use_global_device_ids=true, to_apply=%region_20.0 | all-reduce | flops 1 | bytes 8 | tf_op jit(solution)/shard_map/psum | solution.py:170
  (93 shorter events, 13.4 us)
Async XLA Ops:
  7.2 140.0 %copy-start = (bf16[1024,1024]{1,0:T(8,128)(2,1)S(1)}, bf16[1024,1024]{1,0:T(8,128)(2,1)}, u32[]{:S(2)}) copy-start(bf16[1024,1024]{1,0:T(8,128)(2,1)} %param.20) | copy-start | bytes 6291460
  7.2 195.5 %all-reduce.3.cloned.1.call-start = ((), (), s32[]{:S(2)}) async-start(), calls=%async_computation | async-start | bytes 2097152 | tf_op jit(solution)/shard_map/psum | solution.py:148
  10.6 1.6 copy-start.17
  10.7 13.1 %copy-start.16 = (bf16[128,1024]{1,0:T(8,128)(2,1)}, bf16[128,1024]{1,0:T(8,128)(2,1)S(1)}, u32[]{:S(2)}) copy-start(bf16[128,1024]{1,0:T(8,128)(2,1)S(1)} %get-tuple-element.31) | copy-start | bytes 786436
  51.6 2.2 copy-start.1
  68.8 3.5 copy-start.13
  72.7 25.5 %collective-permute-start = (f32[256,1024]{1,0:T(8,128)S(1)}, f32[256,1024]{1,0:T(8,128)S(1)}, u32[]{:S(2)}, u32[]{:S(2)}) collective-permute-start(f32[256,1024]{1,0:T(8,128)S(1)} %fusion.77), channel_id=1, source_target_pairs={{0,1},{1,0},{2,3},{3,2},{4,5},{5,4},{6,7},{7,6},{8,9},{9,8},{10,11... | collective-permute-start | bytes 3145736 | tf_op jit(solution)/shard_map/ppermute | solution.py:136
  98.3 48.2 %copy-start.3 = (bf16[128,1024]{1,0:T(8,128)(2,1)S(1)}, bf16[128,1024]{1,0:T(8,128)(2,1)}, u32[]{:S(2)}) copy-start(bf16[128,1024]{1,0:T(8,128)(2,1)} %param.12) | copy-start | bytes 786436
  98.3 48.2 %copy-start.10 = (bf16[128,1024]{1,0:T(8,128)(2,1)S(1)}, bf16[128,1024]{1,0:T(8,128)(2,1)}, u32[]{:S(2)}) copy-start(bf16[128,1024]{1,0:T(8,128)(2,1)} %param.11) | copy-start | bytes 786436
  98.3 48.5 %copy-start.21 = (f32[1024]{0:T(1024)S(1)}, f32[1024]{0:T(1024)}, u32[]{:S(2)}) copy-start(f32[1024]{0:T(1024)} %param.19) | copy-start | bytes 12292
  98.4 48.0 %collective-permute-start.1 = (f32[256,1024]{1,0:T(8,128)S(1)}, f32[256,1024]{1,0:T(8,128)S(1)}, u32[]{:S(2)}, u32[]{:S(2)}) collective-permute-start(f32[256,1024]{1,0:T(8,128)S(1)} %add.163), channel_id=1, source_target_pairs={{0,2},{1,3},{2,0},{3,1},{4,6},{5,7},{6,4},{7,5},{8,10},{9,11},{10,... | collective-permute-start | bytes 3145736 | tf_op jit(solution)/shard_map/ppermute | solution.py:136
  147.1 1.6 copy-start.6
  150.4 53.7 %copy-start.20 = (f32[1024]{0:T(1024)S(1)}, f32[1024]{0:T(1024)}, u32[]{:S(2)}) copy-start(f32[1024]{0:T(1024)} %param.14) | copy-start | bytes 12292
  150.4 252.9 %all-reduce.5.cloned.1.call-start = ((), (), s32[]{:S(2)}) async-start(), calls=%async_computation.1 | async-start | bytes 2097152 | tf_op jit(solution)/shard_map/psum | solution.py:148
  202.6 1.8 copy-start.22
  202.6 2.1 copy-start.23
  204.1 1.7 copy-start.8
  204.1 1.6 copy-start.24
  219.6 3.8 copy-start.12
  251.5 2.2 copy-start.2
  253.7 3.4 copy-start.11
  257.1 2.3 copy-start.18
  272.1 2.4 copy-start.14
  272.1 2.4 copy-start.19
  274.8 25.5 %collective-permute-start.2 = (f32[256,1024]{1,0:T(8,128)S(1)}, f32[256,1024]{1,0:T(8,128)S(1)}, u32[]{:S(2)}, u32[]{:S(2)}) collective-permute-start(f32[256,1024]{1,0:T(8,128)S(1)} %fusion.81), channel_id=1, source_target_pairs={{0,1},{1,0},{2,3},{3,2},{4,5},{5,4},{6,7},{7,6},{8,9},{9,8},{10,11... | collective-permute-start | bytes 3145736 | tf_op jit(solution)/shard_map/ppermute | solution.py:136
  300.5 48.2 %copy-start.9 = (f32[128,1024]{1,0:T(8,128)S(1)}, f32[128,1024]{1,0:T(8,128)}, u32[]{:S(2)}) copy-start(f32[128,1024]{1,0:T(8,128)} %copy-done.8) | copy-start | bytes 1572868
  300.5 48.2 %copy-start.15 = (f32[256,1024]{1,0:T(8,128)S(1)}, f32[256,1024]{1,0:T(8,128)}, u32[]{:S(2)}) copy-start(f32[256,1024]{1,0:T(8,128)} %all-reduce.3.cloned.1.call-done) | copy-start | bytes 3145732
  300.5 48.0 %collective-permute-start.3 = (f32[256,1024]{1,0:T(8,128)S(1)}, f32[256,1024]{1,0:T(8,128)S(1)}, u32[]{:S(2)}, u32[]{:S(2)}) collective-permute-start(f32[256,1024]{1,0:T(8,128)S(1)} %add.180), channel_id=1, source_target_pairs={{0,2},{1,3},{2,0},{3,1},{4,6},{5,7},{6,4},{7,5},{8,10},{9,11},{10,... | collective-permute-start | bytes 3145736 | tf_op jit(solution)/shard_map/ppermute | solution.py:136
  348.7 1.0 copy-start.4
  349.7 1.6 copy-start.7
  351.3 52.1 %copy-start.5 = (f32[256,1024]{1,0:T(8,128)S(1)}, f32[256,1024]{1,0:T(8,128)}, u32[]{:S(2)}) copy-start(f32[256,1024]{1,0:T(8,128)} %copy-done.4) | copy-start | bytes 3145732
Sparse Core Ops, SparseCore 0:
  150.6 52.0 all-reduce.2
  353.1 50.2 all-reduce.4
